TPU v7x, 32 devices: a whole 2x2x4 slice. The times are simulated.
32 devices in a mesh: cuts: 8 (over z, y), event: 4 (over x, core).
Axes of the slice: x: 2, y: 2, z: 4, core: 2. Of those that a mesh axis runs over, the one named last changes fastest.
Arguments:
- kernels: float32 [4, 64, 128, 256], P('event', 'cuts'), may hold values from -24 to 24
- steps: float32 [8, 64, 128, 256], P(None, 'cuts', 'event'), may hold values from -11 to 11
- curvature: float32 [8, 64, 128, 256], P(None, 'cuts', 'event'), may hold values from 0.2 to 5
Outputs:
- gradient: float32 [64, 128, 256], P('cuts', 'event')
- direction: float32 [64, 128, 256], P('cuts', 'event')
All inputs are finite; a program needn't handle non-finite values.
Results may differ from a plain program's by a relative error of at most 0.00021.
Values sent between devices are 32-bit elements; how exact they have to be, the bound alone decides.
A program may use at most 64 MiB of HBM per device.

v0:
```python
import math
import jax
import jax.numpy as jnp
from jax import lax
from jax.sharding import PartitionSpec as P

PAIRS = 8
RIM = 4


def with_halo(cells, sides, width):
    for axis, dim in sides:
        count = lax.axis_size(axis)
        head = lax.slice_in_dim(cells, 0, width, axis=dim)
        tail = lax.slice_in_dim(cells, cells.shape[dim] - width, cells.shape[dim], axis=dim)
        cells = jnp.concatenate(
            [
                lax.ppermute(tail, axis, [(i, (i + 1) % count) for i in range(count)]),
                cells,
                lax.ppermute(head, axis, [((i + 1) % count, i) for i in range(count)]),
            ],
            axis=dim,
        )
    return cells


def gauss_matrix(length, sigma):
    points = jnp.arange(length, dtype=jnp.float32)
    offset = points[:, None] - points[None, :]
    matrix = jnp.exp(-offset * offset / (2.0 * sigma * sigma))
    return matrix / jnp.sum(matrix, axis=1, keepdims=True)


def cycle_weights():
    unscaled = [math.exp(-((column - RIM) ** 2) / 4.5) for column in range(2 * RIM + 1)]
    whole = sum(unscaled)
    return [weight / whole for weight in unscaled]


def smooth_plane(field):
    lat_len = field.shape[2]
    plane = jnp.dot(
        field.reshape(-1, lat_len), gauss_matrix(lat_len, 4.0).T, precision=lax.Precision.HIGHEST
    ).reshape(field.shape)
    padded = with_halo(plane, (("cuts", 0),), RIM)
    lon_len = plane.shape[0]
    weights = cycle_weights()
    smoothed = jnp.zeros_like(plane)
    for column in range(2 * RIM + 1):
        smoothed = smoothed + weights[column] * padded[column : column + lon_len]
    return smoothed


def shards(kernels, steps, curvature):
    partial_value = kernels[0]
    rad_len = partial_value.shape[1]
    radial = jnp.einsum(
        "ij,ajb->aib", gauss_matrix(rad_len, 3.0), partial_value, precision=lax.Precision.HIGHEST
    )
    summed = lax.psum(radial, "event")
    smoothed = smooth_plane(summed)
    portion = rad_len // lax.axis_size("event")
    gradient = lax.dynamic_slice_in_dim(smoothed, lax.axis_index("event") * portion, portion, 1)
    changes = curvature * steps
    vectors = jnp.concatenate(
        [steps.reshape(PAIRS, -1), changes.reshape(PAIRS, -1), gradient.reshape(1, -1)], axis=0
    )
    products = lax.psum(
        jnp.dot(vectors, vectors.T, precision=lax.Precision.HIGHEST), ("cuts", "event")
    )
    curvs = jnp.diagonal(products[:PAIRS, PAIRS : 2 * PAIRS])
    inverse = 1.0 / curvs
    scaling = curvs[PAIRS - 1] / products[2 * PAIRS - 1, 2 * PAIRS - 1]
    weights_now = jnp.zeros((2 * PAIRS + 1,), jnp.float32).at[2 * PAIRS].set(1.0)
    alphas = [None] * PAIRS
    for pair in reversed(range(PAIRS)):
        alphas[pair] = inverse[pair] * jnp.dot(
            products[pair], weights_now, precision=lax.Precision.HIGHEST
        )
        weights_now = weights_now.at[PAIRS + pair].add(-alphas[pair])
    weights_now = scaling * weights_now
    for pair in range(PAIRS):
        second = inverse[pair] * jnp.dot(
            products[PAIRS + pair], weights_now, precision=lax.Precision.HIGHEST
        )
        weights_now = weights_now.at[pair].add(alphas[pair] - second)
    direction = -jnp.dot(weights_now[None, :], vectors, precision=lax.Precision.HIGHEST).reshape(
        gradient.shape
    )
    return (gradient, direction)


def solution(mesh):
    placed = (
        P("event", "cuts", None, None),
        P(None, "cuts", "event", None),
        P(None, "cuts", "event", None),
    )
    return jax.shard_map(
        shards,
        mesh=mesh,
        in_specs=placed,
        out_specs=(P("cuts", "event", None), P("cuts", "event", None)),
        check_vma=False,
    )
```

profile of v0, /device:TPU:0, one launch (start us, length us, event | category | flops | bytes accessed | tf_op | source)
XLA Modules:
  0.0 200.9 jit_solution(306684947524946787)
XLA Ops:
  7.2 0.0 copy-start
  7.2 0.0 all-reduce.2.cloned.1.call-start
  7.2 0.1 fusion.36
  7.4 1.0 copy-done
  8.4 2.0 %fusion.11 = f32[128,8,256]{2,0,1:T(8,128)} fusion(f32[1,8,128,256]{3,2,1,0:T(8,128)S(1)} %copy-done, f32[128]{0:T(128)S(1)} %fusion.36), kind=kOutput, calls=%fused_computation.27 | convolution fusion | flops 402735104 | bytes 2097664 | tf_op jit(solution)/shard_map/ij,ajb->aib/dot_general | solution.py:57
  10.4 0.0 all-reduce.2.cloned.1.call-update
  10.5 1.2 copy.40
  11.7 1.5 constant_dynamic-update-slice_fusion.1
  13.2 0.4 mul.113
  13.6 2.6 %copy.41 = f32[1,8,256,256]{3,1,2,0:T(8,128)} copy(f32[1,8,256,256]{3,2,1,0:T(8,128)S(1)} %bitcast.165) | data formatting | bytes 4194304
  16.2 0.2 fusion.28
  16.4 33.3 %all-reduce.2.cloned.1.call-done = f32[1024,256]{1,0:T(8,128)} async-done(((f32[1024,256]{1,0:T(8,128)}), f32[1024,256]{1,0:T(8,128)}) %all-reduce.2.cloned.1.call-update) | async-done | bytes 1048592 | tf_op jit(solution)/shard_map/psum | solution.py:60
  49.6 2.5 %fusion.25 = f32[1024,256]{1,0:T(8,128)S(1)} fusion(f32[1024,256]{1,0:T(8,128)} %all-reduce.2.cloned.1.call-done, f32[256]{0:T(256)S(1)} %fusion.28), kind=kOutput, calls=%fused_computation.48 | convolution fusion | flops 805634048 | bytes 2098176 | tf_op jit(solution)/shard_map/dot_general | solution.py:42
  52.1 0.9 fusion.74
  53.0 1.5 collective-permute-start
  54.5 3.2 %collective-permute-start.1 = (f32[4,128,256]{2,1,0:T(8,128)}, f32[4,128,256]{2,1,0:T(8,128)S(1)}, u32[]{:S(2)}, u32[]{:S(2)}) collective-permute-start(f32[4,128,256]{2,1,0:T(8,128)} %bitcast.6), channel_id=1, source_target_pairs={{4,0},{8,4},{12,8},{16,12},{20,16},{24,20},{28,24},{0,28},{5,1},{9... | collective-permute-start | bytes 1572872 | tf_op jit(solution)/shard_map/ppermute | solution.py:20
  57.7 1.4 constant_dynamic-update-slice_fusion
  59.2 19.6 %collective-permute-done.1 = f32[4,128,256]{2,1,0:T(8,128)S(1)} collective-permute-done((f32[4,128,256]{2,1,0:T(8,128)}, f32[4,128,256]{2,1,0:T(8,128)S(1)}, u32[]{:S(2)}, u32[]{:S(2)}) %collective-permute-start.1) | collective-permute-done | bytes 524320 | tf_op jit(solution)/shard_map/ppermute | solution.py:20
  78.7 0.3 pad_slice_fusion.4
  79.1 2.1 %fusion.4 = (f32[8,128,256]{2,1,0:T(8,128)S(1)}, f32[8,128,256]{2,1,0:T(8,128)S(1)}, f32[8,128,256]{2,1,0:T(8,128)S(1)}, f32[8,128,256]{2,1,0:T(8,128)S(1)}, f32[8,128,256]{2,1,0:T(8,128)S(1)}) fusion(f32[8,128,256]{2,1,0:T(8,128)S(1)} %bitcast.161, f32[4,128,256]{2,1,0:T(8,128)} %collective-permute-done), kind=kLoop, calls=%fused_computation.17 | loop fusion | flops 2621440 | bytes 6815744 | tf_op jit(solution)/shard_map/add | solution.py:50
  81.2 0.2 fusion.17
  81.4 0.3 reshape.412
  81.7 6.0 %dynamic-update-slice.38 = f32[17,65536]{1,0:T(8,128)} dynamic-update-slice(f32[17,65536]{1,0:T(8,128)} %constant_dynamic-update-slice_fusion, f32[1,65536]{1,0:T(1,128)S(1)} %reshape.412, s32[]{} %constant.465, s32[]{} %constant.463) | dynamic-update-slice | bytes 524292 | tf_op jit(solution)/shard_map/concatenate | solution.py:65
  87.7 8.8 %fusion.76 = f32[17,17]{1,0:T(8,128)S(1)} fusion(f32[17,65536]{1,0:T(8,128)} %dynamic-update-slice.38), kind=kOutput, calls=%fused_computation.135 | convolution fusion | flops 227278848 | bytes 4457604 | tf_op jit(solution)/shard_map/dot_general | solution.py:69
  96.5 39.4 %psum.15 = f32[17,17]{1,0:T(8,128)S(1)} all-reduce(f32[17,17]{1,0:T(8,128)S(1)} %fusion.76), channel_id=1, replica_groups=mesh['cuts'=8,'event'=4] {'cuts','event'}, use_global_device_ids=true, to_apply=%region_3.0 | all-reduce | flops 289 | bytes 2312 | tf_op jit(solution)/shard_map/psum | solution.py:68
  135.9 0.1 slice.401
  136.0 0.6 gather_fusion
  136.6 0.6 slice.344
  137.2 0.6 slice.402
  137.8 0.7 fusion.75
  138.5 0.6 fusion.70
  140.3 1.3 fusion.68
  142.9 0.2 constant_dynamic-update-slice_fusion.14
  143.1 1.3 fusion.66
  145.7 0.2 constant_dynamic-update-slice_fusion.13
  145.8 1.3 fusion.64
  148.4 0.2 constant_dynamic-update-slice_fusion.12
  148.6 1.3 fusion.62
  151.1 0.2 constant_dynamic-update-slice_fusion.11
  151.3 1.3 fusion.60
  153.9 0.2 constant_dynamic-update-slice_fusion.10
  154.1 1.3 fusion.58
  156.6 0.2 constant_dynamic-update-slice_fusion.9
  156.8 1.3 fusion.56
  159.4 0.2 constant_dynamic-update-slice_fusion.8
  160.7 1.3 fusion.54
  163.2 1.3 fusion.52
  165.8 0.2 constant_dynamic-update-slice_fusion.7
  166.0 1.4 fusion.50
  168.6 0.2 constant_dynamic-update-slice_fusion.6
  168.8 1.4 fusion.48
  171.4 0.2 add_dynamic-update-slice_fusion.1
  171.6 1.3 fusion.46
  174.1 0.2 constant_dynamic-update-slice_fusion.5
  174.2 1.3 fusion.44
  176.8 0.2 constant_dynamic-update-slice_fusion.4
  177.0 1.4 fusion.42
  179.6 0.2 constant_dynamic-update-slice_fusion.3
  179.7 1.3 fusion.40
  182.3 0.2 add_dynamic-update-slice_fusion
  182.4 4.8 %copy.42 = f32[3,8,256,256]{3,2,1,0:T(8,128)S(1)} copy(f32[3,8,256,256]{3,1,2,0:T(8,128)} %bitcast.159) | data formatting | bytes 12582912
  187.2 0.4 slice.419
  187.7 5.6 %fusion = f32[1,8,32,256]{3,0,2,1:T(1,128)S(1)} fusion(f32[8,32,256,17]{2,1,0,3:T(8,128)S(1)} %bitcast.160, f32[17]{0:T(128)S(1)} %add_dynamic-update-slice_fusion), kind=kOutput, calls=%fused_computation.1 | convolution fusion | flops 13369344 | bytes 4718660 | tf_op jit(solution)/shard_map/dot_general | solution.py:87
  193.3 0.7 bitcast_negate_fusion
  (18 shorter events, 0.1 us)
Async XLA Ops:
  7.2 1.2 copy-start
  7.2 3.3 %copy-start.1 = (f32[8,8,32,256]{3,2,1,0:T(8,128)S(1)}, f32[8,8,32,256]{3,2,1,0:T(8,128)}, u32[]{:S(2)}) copy-start(f32[8,8,32,256]{3,2,1,0:T(8,128)} %param.38) | copy-start | bytes 6291460
  7.2 42.4 %all-reduce.2.cloned.1.call-start = ((), (), s32[]{:S(2)}) async-start(), calls=%async_computation | async-start | bytes 2097152 | tf_op jit(solution)/shard_map/psum | solution.py:60
  10.5 2.7 %copy-start.3 = (f32[8,8,32,256]{3,2,1,0:T(8,128)S(1)}, f32[8,8,32,256]{3,2,1,0:T(8,128)}, u32[]{:S(2)}) copy-start(f32[8,8,32,256]{3,2,1,0:T(8,128)} %param.39) | copy-start | bytes 6291460
  16.2 43.0 %copy-start.6 = (f32[17]{0:T(128)S(1)}, f32[17]{0:T(128)}, u32[]{:S(2)}) copy-start(f32[17]{0:T(128)} %constant.416.clone.1) | copy-start | bytes 208
  49.6 8.1 %copy-start.2 = (f32[1,8,256,256]{3,1,2,0:T(8,128)S(1)}, f32[1,8,256,256]{3,1,2,0:T(8,128)}, u32[]{:S(2)}) copy-start(f32[1,8,256,256]{3,1,2,0:T(8,128)} %copy.41) | copy-start | bytes 6291460
  53.0 26.0 %collective-permute-start = (f32[4,128,256]{2,1,0:T(8,128)S(1)}, f32[4,128,256]{2,1,0:T(8,128)}, u32[]{:S(2)}, u32[]{:S(2)}) collective-permute-start(f32[4,128,256]{2,1,0:T(8,128)S(1)} %bitcast.169), channel_id=1, source_target_pairs={{0,4},{4,8},{8,12},{12,16},{16,20},{20,24},{24,28},{28,0},{1,5},{5... | collective-permute-start | bytes 1572872 | tf_op jit(solution)/shard_map/ppermute | solution.py:18
  54.5 24.2 %collective-permute-start.1 = (f32[4,128,256]{2,1,0:T(8,128)}, f32[4,128,256]{2,1,0:T(8,128)S(1)}, u32[]{:S(2)}, u32[]{:S(2)}) collective-permute-start(f32[4,128,256]{2,1,0:T(8,128)} %bitcast.6), channel_id=1, source_target_pairs={{4,0},{8,4},{12,8},{16,12},{20,16},{24,20},{28,24},{0,28},{5,1},{9... | collective-permute-start | bytes 1572872 | tf_op jit(solution)/shard_map/ppermute | solution.py:20
  81.4 15.1 %copy-start.4 = (f32[8,32,256]{2,1,0:T(8,128)}, f32[8,32,256]{2,1,0:T(8,128)S(1)}, u32[]{:S(2)}) copy-start(f32[8,32,256]{2,1,0:T(8,128)S(1)} %fusion.17) | copy-start | bytes 786436
  135.9 4.4 %copy-start.5 = (f32[17,17]{1,0:T(8,128)}, f32[17,17]{1,0:T(8,128)S(1)}, u32[]{:S(2)}) copy-start(f32[17,17]{1,0:T(8,128)S(1)} %psum.15) | copy-start | bytes 3472
Sparse Core Ops, SparseCore 0:
  10.6 39.0 all-reduce.1
where the time goes:
time: 202 us; the launch traced here: 201 us
  waiting for transfers between devices  52.8 us (26%)
  blocking collectives  39.4 us (20%)
  between operations  35.5 us (18%)
  other arithmetic  26.4 us (13%)
  local copies, waits for them, and re-layouts  23.1 us (11%)
  matrix products  18.9 us (9%)
  starting transfers between devices  4.76 us (2%)
    psum x1, blocking collectives, shards(): lax.psum(jnp.dot(vectors, vectors.T, precision=lax.Precision.HIGHEST), ('...  39.4 us
    psum x1, waiting for transfers between devices, shards(): summed = lax.psum(radial, 'event')  33.3 us
    ppermute x1, waiting for transfers between devices, with_halo(): lax.ppermute(head, axis, [((i + 1) % count, i) for i in range(count)])  19.6 us
    unnamed x21, local copies, waits for them, and re-layouts  13 us
    dot_general x8, other arithmetic, shards(): jnp.dot(products[PAIRS + pair], weights_now, precision=lax.Precision.HIGH...  10.6 us
    dot_general x8, other arithmetic, shards(): jnp.dot(products[pair], weights_now, precision=lax.Precision.HIGHEST)  9.85 us
    dot_general x1, matrix products, shards(): jnp.dot(vectors, vectors.T, precision=lax.Precision.HIGHEST)  8.77 us
    concatenate x1, local copies, waits for them, and re-layouts, shards(): jnp.concatenate([steps.reshape(PAIRS, -1), changes.reshape(PAIRS, -1), gr...  6.03 us
  transfers between devices with their start and end apart: 3, of which 2 were waited for; matrix products, arithmetic and copies ran while one was open for 4% of the time, Pallas kernels for 0%

commit v1 on v0

--- a/solution.py
+++ b/solution.py
@@ -65,8 +65,11 @@
     vectors = jnp.concatenate(
         [steps.reshape(PAIRS, -1), changes.reshape(PAIRS, -1), gradient.reshape(1, -1)], axis=0
     )
-    products = lax.psum(
-        jnp.dot(vectors, vectors.T, precision=lax.Precision.HIGHEST), ("cuts", "event")
+    _connect_seats_all = lambda base_x, group_axis, chip_axis: lax.psum(
+        lax.psum(base_x, group_axis), chip_axis
+    )
+    products = _connect_seats_all(
+        jnp.dot(vectors, vectors.T, precision=lax.Precision.HIGHEST), "event", "cuts"
     )
     curvs = jnp.diagonal(products[:PAIRS, PAIRS : 2 * PAIRS])
     inverse = 1.0 / curvs

time: 202 us -> 209 us (1.035)
  blocking collectives: 39.4 us -> 46.6 us
    psum x1 -> x2, blocking collectives: 39.4 us -> 46.6 us  [the longest x1 36.4 us: shards(): lax.psum(lax.psum(base_x, group_axis), chip_axis)]
where the time goes in v1:
time: 209 us; the launch traced here: 208 us
  waiting for transfers between devices  52.8 us (25%)
  blocking collectives  46.6 us (22%)
  between operations  35.5 us (17%)
  other arithmetic  26.4 us (13%)
  local copies, waits for them, and re-layouts  23.1 us (11%)
  matrix products  18.9 us (9%)
  starting transfers between devices  4.76 us (2%)
    psum x1, blocking collectives, shards(): lax.psum(lax.psum(base_x, group_axis), chip_axis)  36.4 us
    psum x1, waiting for transfers between devices, shards(): summed = lax.psum(radial, 'event')  33.3 us
    ppermute x1, waiting for transfers between devices, with_halo(): lax.ppermute(head, axis, [((i + 1) % count, i) for i in range(count)])  19.6 us
    unnamed x21, local copies, waits for them, and re-layouts  13 us
    dot_general x8, other arithmetic, shards(): jnp.dot(products[PAIRS + pair], weights_now, precision=lax.Precision.HIGH...  10.6 us
    psum x1, blocking collectives, shards(): lax.psum(base_x, group_axis)  10.1 us
    dot_general x8, other arithmetic, shards(): jnp.dot(products[pair], weights_now, precision=lax.Precision.HIGHEST)  9.85 us
    dot_general x1, matrix products, shards(): jnp.dot(vectors, vectors.T, precision=lax.Precision.HIGHEST)  8.77 us
  transfers between devices with their start and end apart: 3, of which 2 were waited for; matrix products, arithmetic and copies ran while one was open for 4% of the time, Pallas kernels for 0%

profile of v1, /device:TPU:0, one launch (start us, length us, event | category | flops | bytes accessed | tf_op | source)
XLA Modules:
  0.0 208.0 jit_solution(7003556124055098034)
XLA Ops:
  7.2 0.0 all-reduce.2.cloned.1.call-start
  7.2 0.1 fusion.36
  7.4 1.0 copy-done
  8.4 2.0 fusion.11
  10.4 0.0 all-reduce.2.cloned.1.call-update
  10.5 1.2 copy.40
  11.7 1.5 constant_dynamic-update-slice_fusion.1
  13.2 0.4 mul.113
  13.6 2.6 %copy.41 = f32[1,8,256,256]{3,1,2,0:T(8,128)} copy(f32[1,8,256,256]{3,2,1,0:T(8,128)S(1)} %bitcast.165) | data formatting | bytes 4194304
  16.2 0.2 fusion.28
  16.4 33.3 %all-reduce.2.cloned.1.call-done = f32[1024,256]{1,0:T(8,128)} async-done(((f32[1024,256]{1,0:T(8,128)}), f32[1024,256]{1,0:T(8,128)}) %all-reduce.2.cloned.1.call-update) | async-done | bytes 1048592 | tf_op jit(solution)/shard_map/psum | solution.py:60
  49.6 2.5 %fusion.25 = f32[1024,256]{1,0:T(8,128)S(1)} fusion(f32[1024,256]{1,0:T(8,128)} %all-reduce.2.cloned.1.call-done, f32[256]{0:T(256)S(1)} %fusion.28), kind=kOutput, calls=%fused_computation.48 | convolution fusion | flops 805634048 | bytes 2098176 | tf_op jit(solution)/shard_map/dot_general | solution.py:42
  52.1 0.9 fusion.74
  53.0 1.5 collective-permute-start
  54.5 3.2 %collective-permute-start.1 = (f32[4,128,256]{2,1,0:T(8,128)}, f32[4,128,256]{2,1,0:T(8,128)S(1)}, u32[]{:S(2)}, u32[]{:S(2)}) collective-permute-start(f32[4,128,256]{2,1,0:T(8,128)} %bitcast.6), channel_id=1, source_target_pairs={{4,0},{8,4},{12,8},{16,12},{20,16},{24,20},{28,24},{0,28},{5,1},{9... | collective-permute-start | bytes 1572872 | tf_op jit(solution)/shard_map/ppermute | solution.py:20
  57.7 1.4 constant_dynamic-update-slice_fusion
  59.2 19.6 %collective-permute-done.1 = f32[4,128,256]{2,1,0:T(8,128)S(1)} collective-permute-done((f32[4,128,256]{2,1,0:T(8,128)}, f32[4,128,256]{2,1,0:T(8,128)S(1)}, u32[]{:S(2)}, u32[]{:S(2)}) %collective-permute-start.1) | collective-permute-done | bytes 524320 | tf_op jit(solution)/shard_map/ppermute | solution.py:20
  78.7 0.3 pad_slice_fusion.4
  79.1 2.1 %fusion.4 = (f32[8,128,256]{2,1,0:T(8,128)S(1)}, f32[8,128,256]{2,1,0:T(8,128)S(1)}, f32[8,128,256]{2,1,0:T(8,128)S(1)}, f32[8,128,256]{2,1,0:T(8,128)S(1)}, f32[8,128,256]{2,1,0:T(8,128)S(1)}) fusion(f32[8,128,256]{2,1,0:T(8,128)S(1)} %bitcast.161, f32[4,128,256]{2,1,0:T(8,128)} %collective-permute-done), kind=kLoop, calls=%fused_computation.17 | loop fusion | flops 2621440 | bytes 6815744 | tf_op jit(solution)/shard_map/add | solution.py:50
  81.2 0.2 fusion.17
  81.4 0.3 reshape.412
  81.7 6.0 %dynamic-update-slice.38 = f32[17,65536]{1,0:T(8,128)} dynamic-update-slice(f32[17,65536]{1,0:T(8,128)} %constant_dynamic-update-slice_fusion, f32[1,65536]{1,0:T(1,128)S(1)} %reshape.412, s32[]{} %constant.465, s32[]{} %constant.463) | dynamic-update-slice | bytes 524292 | tf_op jit(solution)/shard_map/concatenate | solution.py:65
  87.7 8.8 %fusion.76 = f32[17,17]{1,0:T(8,128)S(1)} fusion(f32[17,65536]{1,0:T(8,128)} %dynamic-update-slice.38), kind=kOutput, calls=%fused_computation.135 | convolution fusion | flops 227278848 | bytes 4457604 | tf_op jit(solution)/shard_map/dot_general | solution.py:72
  96.5 10.1 %psum.22 = f32[17,17]{1,0:T(8,128)S(1)} all-reduce(f32[17,17]{1,0:T(8,128)S(1)} %fusion.76), channel_id=1, replica_groups=mesh['cuts'=8,'event'=4] {'event'}, use_global_device_ids=true, to_apply=%region_3.0 | all-reduce | flops 289 | bytes 2312 | tf_op jit(solution)/shard_map/psum | solution.py:69
  106.6 36.4 %psum.23 = f32[17,17]{1,0:T(8,128)S(1)} all-reduce(f32[17,17]{1,0:T(8,128)S(1)} %psum.22), channel_id=1, replica_groups=mesh['cuts'=8,'event'=4] {'cuts'}, use_global_device_ids=true, to_apply=%region_4.0 | all-reduce | flops 289 | bytes 2312 | tf_op jit(solution)/shard_map/psum | solution.py:68
  143.1 0.1 slice.401
  143.2 0.6 gather_fusion
  143.8 0.6 slice.344
  144.4 0.6 slice.402
  144.9 0.7 fusion.75
  145.6 0.6 fusion.70
  147.5 1.3 fusion.68
  150.1 0.2 constant_dynamic-update-slice_fusion.14
  150.2 1.3 fusion.66
  152.8 0.2 constant_dynamic-update-slice_fusion.13
  153.0 1.3 fusion.64
  155.6 0.2 constant_dynamic-update-slice_fusion.12
  155.7 1.3 fusion.62
  158.3 0.2 constant_dynamic-update-slice_fusion.11
  158.4 1.3 fusion.60
  161.1 0.2 constant_dynamic-update-slice_fusion.10
  161.2 1.3 fusion.58
  163.8 0.2 constant_dynamic-update-slice_fusion.9
  163.9 1.3 fusion.56
  166.5 0.2 constant_dynamic-update-slice_fusion.8
  167.9 1.3 fusion.54
  170.4 1.3 fusion.52
  172.9 0.2 constant_dynamic-update-slice_fusion.7
  173.1 1.4 fusion.50
  175.8 0.2 constant_dynamic-update-slice_fusion.6
  175.9 1.4 fusion.48
  178.6 0.2 add_dynamic-update-slice_fusion.1
  178.7 1.3 fusion.46
  181.2 0.2 constant_dynamic-update-slice_fusion.5
  181.4 1.3 fusion.44
  184.0 0.2 constant_dynamic-update-slice_fusion.4
  184.1 1.4 fusion.42
  186.7 0.2 constant_dynamic-update-slice_fusion.3
  186.9 1.3 fusion.40
  189.4 0.2 add_dynamic-update-slice_fusion
  189.6 4.8 %copy.42 = f32[3,8,256,256]{3,2,1,0:T(8,128)S(1)} copy(f32[3,8,256,256]{3,1,2,0:T(8,128)} %bitcast.159) | data formatting | bytes 12582912
  194.4 0.4 slice.419
  194.8 5.6 %fusion = f32[1,8,32,256]{3,0,2,1:T(1,128)S(1)} fusion(f32[8,32,256,17]{2,1,0,3:T(8,128)S(1)} %bitcast.160, f32[17]{0:T(128)S(1)} %add_dynamic-update-slice_fusion), kind=kOutput, calls=%fused_computation.1 | convolution fusion | flops 13369344 | bytes 4718660 | tf_op jit(solution)/shard_map/dot_general | solution.py:90
  200.4 0.7 bitcast_negate_fusion
  (19 shorter events, 0.1 us)
Async XLA Ops:
  7.2 1.2 copy-start
  7.2 3.3 %copy-start.1 = (f32[8,8,32,256]{3,2,1,0:T(8,128)S(1)}, f32[8,8,32,256]{3,2,1,0:T(8,128)}, u32[]{:S(2)}) copy-start(f32[8,8,32,256]{3,2,1,0:T(8,128)} %param.38) | copy-start | bytes 6291460
  7.2 42.4 %all-reduce.2.cloned.1.call-start = ((), (), s32[]{:S(2)}) async-start(), calls=%async_computation | async-start | bytes 2097152 | tf_op jit(solution)/shard_map/psum | solution.py:60
  10.5 2.7 %copy-start.3 = (f32[8,8,32,256]{3,2,1,0:T(8,128)S(1)}, f32[8,8,32,256]{3,2,1,0:T(8,128)}, u32[]{:S(2)}) copy-start(f32[8,8,32,256]{3,2,1,0:T(8,128)} %param.39) | copy-start | bytes 6291460
  16.2 43.0 %copy-start.6 = (f32[17]{0:T(128)S(1)}, f32[17]{0:T(128)}, u32[]{:S(2)}) copy-start(f32[17]{0:T(128)} %constant.416.clone.1) | copy-start | bytes 208
  49.6 8.1 %copy-start.2 = (f32[1,8,256,256]{3,1,2,0:T(8,128)S(1)}, f32[1,8,256,256]{3,1,2,0:T(8,128)}, u32[]{:S(2)}) copy-start(f32[1,8,256,256]{3,1,2,0:T(8,128)} %copy.41) | copy-start | bytes 6291460
  53.0 26.0 %collective-permute-start = (f32[4,128,256]{2,1,0:T(8,128)S(1)}, f32[4,128,256]{2,1,0:T(8,128)}, u32[]{:S(2)}, u32[]{:S(2)}) collective-permute-start(f32[4,128,256]{2,1,0:T(8,128)S(1)} %bitcast.169), channel_id=1, source_target_pairs={{0,4},{4,8},{8,12},{12,16},{16,20},{20,24},{24,28},{28,0},{1,5},{5... | collective-permute-start | bytes 1572872 | tf_op jit(solution)/shard_map/ppermute | solution.py:18
  54.5 24.2 %collective-permute-start.1 = (f32[4,128,256]{2,1,0:T(8,128)}, f32[4,128,256]{2,1,0:T(8,128)S(1)}, u32[]{:S(2)}, u32[]{:S(2)}) collective-permute-start(f32[4,128,256]{2,1,0:T(8,128)} %bitcast.6), channel_id=1, source_target_pairs={{4,0},{8,4},{12,8},{16,12},{20,16},{24,20},{28,24},{0,28},{5,1},{9... | collective-permute-start | bytes 1572872 | tf_op jit(solution)/shard_map/ppermute | solution.py:20
  81.4 15.1 %copy-start.4 = (f32[8,32,256]{2,1,0:T(8,128)}, f32[8,32,256]{2,1,0:T(8,128)S(1)}, u32[]{:S(2)}) copy-start(f32[8,32,256]{2,1,0:T(8,128)S(1)} %fusion.17) | copy-start | bytes 786436
  143.1 4.4 %copy-start.5 = (f32[17,17]{1,0:T(8,128)}, f32[17,17]{1,0:T(8,128)S(1)}, u32[]{:S(2)}) copy-start(f32[17,17]{1,0:T(8,128)S(1)} %psum.23) | copy-start | bytes 3472
Sparse Core Ops, SparseCore 0:
  10.6 39.0 all-reduce.1
